TPU v7x, 32 devices: a whole 2x2x4 slice. The times are simulated.
32 devices in a mesh: row: 8 (over y, x, core), grp: 4 (over z).
Axes of the slice: x: 2, y: 2, z: 4, core: 2. Of those that a mesh axis runs over, the one named last changes fastest.
Arguments:
- positions: float32 [3, 1024], replicated, may hold values from -0.05 to 9.35, as said below
- detuning: float32 [1024], replicated, may hold values from -1 to 1
- populations: float32 [1024], P('row'), may hold values from 0 to 1
- base: float32 [2, 64, 1024], P(None, 'grp', 'row'), may hold values from -6 to 6
- section: float32 [2, 64, 1024], P(None, 'grp', 'row'), may hold values from -6 to 6
- accum: float32 [2, 64, 1024], P(None, 'grp', 'row'), may hold values from -3 to 3
Outputs:
- next_input: float32 [2, 64, 1024], P(None, 'grp', 'row')
- accum_out: float32 [2, 64, 1024], P(None, 'grp', 'row')
Inputs may be any that keep to these rules, and one draw needn't show every extreme that they name: `positions`: emitter n sits near the lattice point 0.3 * (n % 32, (n // 32) % 32, n // 1024), displaced by at most 0.05 in each coordinate.
All inputs are finite; a program needn't handle non-finite values.
Results may differ from a plain program's by a relative error of at most 0.0003.
Values sent between devices are 32-bit elements; how exact they have to be, the bound alone decides.
A program may use at most 64 MiB of HBM per device.

v0:
```python
import functools
import math

import jax
import jax.numpy as jnp
from jax import lax
from jax.experimental import pallas as pl
from jax.experimental.pallas import tpu as pltpu
from jax.sharding import PartitionSpec as P

TIME_STEP = 0.2
PAD = 16
TILE = 128
AMPLITUDE = -0.75
PAUSE = 1

HALF_SIN = (4.442882834149929, -7.308241154546326, 3.606288958225646, -0.8457635961475002, 0.10920575363724722)
HALF_COS = (1.4142134965650124, -6.97885098823893, 5.739461170681154, -1.8835629872981716, 0.31069819180355424)
MESH = pl.DeviceIdType.MESH


def horner(coeffs, t):
    total = coeffs[-1] * t + coeffs[-2]
    for value in coeffs[-3::-1]:
        total = total * t + value
    return total


def coupling(cols, rows, diag):
    dx = cols[0] - rows[0]
    dy = cols[1] - rows[1]
    dz = cols[2] - rows[2]
    dz_sq = dz * dz
    dist_sq = dx * dx + dy * dy + dz_sq
    if diag is not None:
        dist_sq = jnp.where(diag, 1.0, dist_sq)
    inv = lax.rsqrt(dist_sq)
    dist = dist_sq * inv
    frac = dist - jnp.round(dist)
    t = frac * frac
    half_sin = frac * horner(HALF_SIN, t)
    half_cos = horner(HALF_COS, t)
    sine = half_sin * half_cos
    cosine = 1.0 - half_sin * half_sin
    u = inv * (0.5 / math.pi)
    aligned = dz_sq * (inv * inv)
    amp_imag = (u * u) * (1.0 - 3.0 * aligned)
    amp_real = u * ((1.0 - aligned) - amp_imag)
    h_real = amp_real * cosine - amp_imag * sine
    h_imag = amp_real * sine + amp_imag * cosine
    if diag is not None:
        h_real = jnp.where(diag, 0.0, h_real)
        h_imag = jnp.where(diag, 0.0, h_imag)
    return h_real, h_imag


def split(x):
    hi = x.astype(jnp.bfloat16)
    return hi, (x - hi.astype(jnp.float32)).astype(jnp.bfloat16)


def bdot(a, b):
    return jnp.dot(a, b, preferred_element_type=jnp.float32)


def exchange(
    n_row,
    n_grp,
    pos_in,
    det_in,
    pop_in,
    sec_in,
    base_in,
    accum_in,
    next_ref,
    accum_ref,
    olds,
    pos_ref,
    det_ref,
    stage,
    wide,
    rhs_hi,
    rhs_lo,
    row_buf,
    grp_buf,
    coef,
    send_sem,
    row_recv,
    grp_recv,
    row_ready,
    grp_ready,
    load_sem,
):
    cols, width = sec_in.shape[0] // 2, sec_in.shape[1]
    me = lax.axis_index("row")
    mine = lax.axis_index("grp")
    slab = cols * n_grp
    barrier = pltpu.get_barrier_semaphore()

    last = n_row - 2
    pair = me // 2
    odd = lax.rem(me, 2)
    partner = me + 1 - 2 * odd
    in_first = me < 2
    in_last = me >= last
    between = jnp.logical_not(in_first | in_last)
    even = odd == 0
    low = jnp.minimum(mine, 1)
    ahead = in_first & even & (mine > 0)
    GO, LATE, WORD = 0, 1, 2
    NEXT, REST = 0, 1

    def to_row(sem, lo, hi):
        def body(p, carry):
            pl.semaphore_signal(sem, inc=1, device_id={"row": p}, device_id_type=MESH)
            return carry

        lax.fori_loop(lo, hi, body, 0)

    def to_grp(sem, lo, hi):
        def body(p, carry):
            pl.semaphore_signal(sem, inc=1, device_id={"grp": p}, device_id_type=MESH)
            return carry

        lax.fori_loop(lo, hi, body, 0)

    slab_part = stage.at[0 : 2 * cols]

    def send_row(lo, hi):
        def body(p, carry):
            pltpu.make_async_remote_copy(
                stage,
                row_buf.at[me],
                send_sem.at[0],
                row_recv.at[jnp.where(me < last, 0, 1)],
                device_id={"row": p},
                device_id_type=MESH,
            ).start()
            return carry

        lax.fori_loop(lo, hi, body, 0)

    def send_grp(lo, hi, source):
        def body(p, carry):
            pltpu.make_async_remote_copy(
                source,
                grp_buf.at[mine],
                send_sem.at[1],
                grp_recv.at[jnp.where(mine < n_grp - 1, 0, 1)],
                device_id={"grp": p},
                device_id_type=MESH,
            ).start()
            return carry

        lax.fori_loop(lo, hi, body, 0)

    def arrived(part, sem):
        pltpu.make_async_copy(part, part, sem).wait()

    @pl.when(ahead)
    def _():
        pl.semaphore_wait(barrier, 1)
        send_grp(0, 1, sec_in)

    section_loads = [
        pltpu.make_async_copy(src, dst, load_sem.at[0])
        for src, dst in (
            (sec_in, stage.at[0 : 2 * cols]),
            (pop_in, stage.at[2 * cols : 2 * cols + 1]),
        )
    ]
    pos_load = pltpu.make_async_copy(pos_in, pos_ref, load_sem.at[1])
    det_load = pltpu.make_async_copy(det_in, det_ref, load_sem.at[2])
    old_loads = [
        pltpu.make_async_copy(src, olds.at[i], load_sem.at[3]) for i, src in enumerate((base_in, accum_in))
    ]
    for load in (*section_loads, pos_load, det_load, *old_loads):
        load.start()

    @pl.when(even & (mine > 0))
    def _():
        def body(p, carry):
            pl.semaphore_signal(barrier, inc=1, device_id={"row": partner, "grp": p}, device_id_type=MESH)
            return carry

        lax.fori_loop(mine + 1, n_grp, body, 0)

    @pl.when(jnp.logical_not(even & (mine > 0)))
    def _():
        to_grp(barrier, mine + 1, n_grp)

    @pl.when(even)
    def _():
        pl.semaphore_signal(barrier, inc=1, device_id={"row": partner}, device_id_type=MESH)

    after = jnp.where(in_first, 2, jnp.where(in_last, n_row, last))
    to_row(barrier, after, n_row)

    before = jnp.where(in_first, 0, jnp.where(in_last, last, 2))
    met = before + jnp.where(even, low, 1 + mine + mine - low)

    @pl.when((met > 0) & jnp.logical_not(ahead))
    def _():
        with jax.named_scope("bar"):
            pl.semaphore_wait(barrier, met)

    send_grp(0, jnp.where(even & jnp.logical_not(ahead), low, 0), sec_in)

    def answer_lower(lo, hi):
        to_grp(grp_ready.at[REST], lo, jnp.minimum(hi, mine - 1))
        to_grp(grp_ready.at[NEXT], jnp.maximum(lo, mine - 1), hi)

    answer_lower(0, low)

    @pl.when(between)
    def _():
        to_row(row_ready.at[GO], 0, 2)

    @pl.when(in_last)
    def _():
        to_row(row_ready.at[LATE], 0, last)

    @pl.when(jnp.logical_not(even))
    def _():
        pl.semaphore_signal(row_ready.at[WORD], inc=1, device_id={"row": partner}, device_id_type=MESH)
        answer_lower(low, mine)

    def hear_between():
        with jax.named_scope("wmid"):
            pl.semaphore_wait(row_ready.at[GO], last - 2)

        @pl.when(odd == 1)
        def _():
            to_row(row_ready.at[GO], 2, last)

    @pl.when(in_first & (mine == 0) & (last > 2))
    def _():
        hear_between()

    with jax.named_scope("load"):
        pos_load.wait()
        arrived(stage, load_sem.at[0])
    send_row(jnp.where(in_first, 2, 0), jnp.where(in_first, jnp.where(mine == 0, last, 2), before))

    @pl.when(even)
    def _():
        with jax.named_scope("word"):
            pl.semaphore_wait(row_ready.at[WORD], 1)
        answer_lower(low, mine)
        send_grp(low, mine, slab_part)

    send_row(partner, partner + 1)

    my_start = pl.multiple_of(me * width, width)
    rows = [pos_ref[d : d + 1, pl.ds(my_start, width)] for d in range(3)]
    tiles = width // TILE

    def spread(tile, slot):
        start = pl.multiple_of(tile * TILE, TILE)
        for d in range(3):
            line = pos_ref[d : d + 1, pl.ds(start, TILE)]
            wide[slot, d] = jnp.transpose(jnp.broadcast_to(line, (TILE, TILE)))

    def fill(tile, slot, diag):
        start = pl.multiple_of(tile * TILE, TILE)
        for part in range(tiles):
            lanes = slice(part * TILE, (part + 1) * TILE)
            h_real, h_imag = coupling(
                [wide[slot, d] for d in range(3)],
                [r[:, lanes] for r in rows],
                None if diag is None else diag[:, lanes],
            )
            for base, h in ((0, h_real), (width, h_imag)):
                hi, lo = split(h)
                at = slice(base + part * TILE, base + (part + 1) * TILE)
                rhs_hi[pl.ds(start, TILE), at] = hi
                rhs_lo[pl.ds(start, TILE), at] = lo

    first = me * tiles
    total = n_row * tiles
    lane_ids = lax.broadcasted_iota(jnp.int32, (TILE, width), 1)
    sub_ids = lax.broadcasted_iota(jnp.int32, (TILE, width), 0)

    def tile_at(j):
        return lax.rem(first + j, total)

    with jax.named_scope("couple"):
        def lower_from_odd():
            @pl.when(jnp.logical_not(even))
            def _():
                send_grp(0, mine, slab_part)

        def step(j, carry):
            spread(tile_at(j + 1), lax.rem(j + 1, 2))
            fill(tile_at(j), lax.rem(j, 2), None)
            return carry

        flat = total <= 16
        spread(first, 0)
        for j in range(total if flat else tiles):
            if j == tiles + PAUSE:
                lower_from_odd()
            if j + 1 < total:
                spread(tile_at(j + 1), (j + 1) % 2)
            fill(tile_at(j), j % 2, sub_ids + j * TILE == lane_ids if j < tiles else None)
        if not flat:
            lower_from_odd()
            lax.fori_loop(tiles, total, step, 0)

    @pl.when(in_first & (mine > 0) & (last > 2))
    def _():
        hear_between()
        send_row(2, last)

    @pl.when(between)
    def _():
        with jax.named_scope("wgo"):
            pl.semaphore_wait(row_ready.at[GO], 1)
        send_row(2, 2 * pair)
        send_row(2 * pair + 2, last)

    @pl.when(mine < n_grp - 1)
    def _():
        with jax.named_scope("ansnext"):
            pl.semaphore_wait(grp_ready.at[NEXT], 1)
        send_grp(mine + 1, mine + 2, slab_part)

    @pl.when(jnp.logical_not(in_last))
    def _():
        with jax.named_scope("wlate"):
            pl.semaphore_wait(row_ready.at[LATE], 2)
        send_row(last, n_row)

    @pl.when(mine < n_grp - 2)
    def _():
        with jax.named_scope("ansrest"):
            pl.semaphore_wait(grp_ready.at[REST], n_grp - 2 - mine)
        send_grp(mine + 2, n_grp, slab_part)

    det_load.wait()
    arrived(olds, load_sem.at[3])

    col_start = pl.multiple_of(mine * cols, cols)
    eye = lax.broadcasted_iota(jnp.int32, (cols, TILE), 0) + col_start == lax.broadcasted_iota(
        jnp.int32, (cols, TILE), 1
    )
    slab_rows = [pos_ref[d : d + 1, :TILE] for d in range(3)]
    own_cols = [
        jnp.sum(jnp.where(eye, jnp.broadcast_to(r, (cols, TILE)), 0.0), axis=1, keepdims=True) for r in slab_rows
    ]
    w_real, w_imag = coupling(own_cols, slab_rows, eye)
    w_real = AMPLITUDE * w_real + jnp.where(eye, det_ref[:, :TILE], 0.0)
    w_imag = AMPLITUDE * w_imag + jnp.where(eye, -0.5, 0.0)
    most = slab - cols
    l_hi, l_lo = split(jnp.concatenate([w_real, w_imag], axis=0)[:, :most])
    for j in range(cols):
        for lead, w in ((0, w_real), (cols, w_imag)):
            coef[j, lead : lead + cols] = jnp.broadcast_to(w[:, most + j : most + j + 1], (cols, width))

    y_local = stage[0 : 2 * cols]
    row_buf[me] = stage[...]
    grp_buf[mine] = y_local

    def left(slab_and_pop):
        signed = jnp.broadcast_to(2.0 * slab_and_pop[2 * cols :] - 1.0, (PAD, width))
        return split(jnp.concatenate([slab_and_pop[: 2 * cols], signed], axis=0))

    main = jnp.zeros((4 * cols + 2 * PAD, 2 * width), jnp.float32)
    rest = jnp.zeros((2 * cols + PAD, 2 * width), jnp.float32)
    group = 2
    for lead in range(0, n_row, group):
        his, los = [], []
        for at, count in ((0, last), (last, 2)):
            if lead == at:
                with jax.named_scope(f"wrow{lead}"):

                    @pl.when(in_last == (at == last))
                    def _():
                        arrived(row_buf.at[0 : count - 1], row_recv.at[at // last])

                    @pl.when(in_last != (at == last))
                    def _():
                        arrived(row_buf.at[0:count], row_recv.at[at // last])

        for p in range(lead, lead + group):
            hi, lo = left(row_buf[p])
            his.append(hi)
            los.append(lo)
        hi = jnp.concatenate(his, axis=1)
        lo = jnp.concatenate(los, axis=1)
        span = slice(lead * width, (lead + group) * width)
        main = main + bdot(jnp.concatenate([hi, lo], axis=0), rhs_hi[span, :])
        rest = rest + bdot(hi, rhs_lo[span, :])
    half = 2 * cols + PAD
    z = AMPLITUDE * (main[:half] + main[half:] + rest)
    z_real = z[:cols, :width] - z[cols : 2 * cols, width:]
    z_imag = z[:cols, width:] + z[cols : 2 * cols, :width]
    shift = z[2 * cols : 2 * cols + 1, :width]

    y_real, y_imag = y_local[:cols], y_local[cols:]
    total_shift = shift + det_ref[:, pl.ds(my_start, width)]
    z_real = z_real + total_shift * y_real + 0.5 * y_imag
    z_imag = z_imag + total_shift * y_imag - 0.5 * y_real

    top = n_grp - 1
    if n_grp > 2:
        with jax.named_scope("wgrp"):

            @pl.when(mine < top)
            def _():
                arrived(grp_buf.at[0 : top - 1], grp_recv.at[0])

            @pl.when(mine == top)
            def _():
                arrived(grp_buf.at[0:top], grp_recv.at[0])

    elif n_grp == 2:

        @pl.when(mine == top)
        def _():
            arrived(grp_buf.at[0:top], grp_recv.at[0])

    blocks = [grp_buf[g] for g in range(top)]
    full = jnp.concatenate(
        [jnp.concatenate([block[:cols], block[cols:]], axis=1) for block in blocks], axis=0
    )
    f_hi, f_lo = split(full)
    v = bdot(l_hi, f_hi) + bdot(l_lo, f_hi) + bdot(l_hi, f_lo)
    z_imag = z_imag - (v[:cols, width:] - v[cols:, :width])
    z_real = z_real - (v[:cols, :width] + v[cols:, width:])

    for i, rate in enumerate((z_imag, -z_real)):
        next_ref[i] = olds[0, i] + 0.5 * TIME_STEP * rate
        accum_ref[i] = olds[1, i] + TIME_STEP / 3.0 * rate

    with jax.named_scope("drain"):
        arrived(row_buf.at[0 : n_row - 1], send_sem.at[0])
        arrived(grp_buf.at[0 : n_grp - 1], send_sem.at[1])


def finish(n_grp, next_ref, accum_ref, grp_buf, coef, grp_recv):
    cols, width = coef.shape[0], coef.shape[2]
    mine, top = lax.axis_index("grp"), n_grp - 1

    with jax.named_scope("wtop"):

        @pl.when(mine < top)
        def _():
            pltpu.make_async_copy(grp_buf.at[0], grp_buf.at[0], grp_recv.at[1]).wait()

    sums = [[jnp.zeros((cols, width), jnp.float32)] * 4 for _ in range(2)]
    for j in range(cols):
        fr = grp_buf[top, j : j + 1]
        fi = grp_buf[top, cols + j : cols + j + 1]
        wr, wi = coef[j, :cols], coef[j, cols:]
        k = 2 * (j % 2)
        sums[0][k] = sums[0][k] + wr * fr
        sums[0][k + 1] = sums[0][k + 1] + wi * fi
        sums[1][k] = sums[1][k] + wr * fi
        sums[1][k + 1] = sums[1][k + 1] + wi * fr
    v_real = (sums[0][0] + sums[0][1]) + (sums[0][2] + sums[0][3])
    v_imag = (sums[1][0] + sums[1][2]) - (sums[1][1] + sums[1][3])
    for i, rate in enumerate((-v_imag, v_real)):
        next_ref[i] = next_ref[i] + 0.5 * TIME_STEP * rate
        accum_ref[i] = accum_ref[i] + TIME_STEP / 3.0 * rate


def kernel(n_row, n_grp, pos_in, det_in, pop_in, sec_in, base_in, accum_in, next_ref, accum_ref, olds, pos_ref, det_ref, stage, wide, rhs_hi, rhs_lo, row_buf, grp_buf, coef):
    def scope(row_recv, grp_recv, row_ready, grp_ready, load_sem, send_sem):
        exchange(n_row=n_row, n_grp=n_grp, pos_in=pos_in, det_in=det_in, pop_in=pop_in, sec_in=sec_in, base_in=base_in, accum_in=accum_in, next_ref=next_ref, accum_ref=accum_ref, olds=olds, pos_ref=pos_ref, det_ref=det_ref, stage=stage, wide=wide, rhs_hi=rhs_hi, rhs_lo=rhs_lo, row_buf=row_buf, grp_buf=grp_buf, coef=coef, row_recv=row_recv, grp_recv=grp_recv, row_ready=row_ready, grp_ready=grp_ready, load_sem=load_sem, send_sem=send_sem)
        finish(n_grp, next_ref, accum_ref, grp_buf, coef, grp_recv)

    pl.run_scoped(
        scope,
        row_recv=pltpu.SemaphoreType.DMA((2,)),
        grp_recv=pltpu.SemaphoreType.DMA((2,)),
        row_ready=pltpu.SemaphoreType.REGULAR((3,)),
        grp_ready=pltpu.SemaphoreType.REGULAR((2,)),
        load_sem=pltpu.SemaphoreType.DMA((4,)),
        send_sem=pltpu.SemaphoreType.DMA((2,)),
    )


def store(next_ref, accum_ref, next_out, accum_out):
    def scope(sem):
        copies = [
            pltpu.make_async_copy(next_ref, next_out, sem.at[0]),
            pltpu.make_async_copy(accum_ref, accum_out, sem.at[1]),
        ]
        for copy in copies:
            copy.start()
        for copy in copies:
            copy.wait()

    pl.run_scoped(scope, pltpu.SemaphoreType.DMA((2,)))


def local(positions, detuning, populations, base, section, accum):
    n_row, n_grp = lax.axis_size("row"), lax.axis_size("grp")
    cols, width = section.shape[1], section.shape[2]
    total = positions.shape[1]
    block = section.shape
    results = pl.pallas_call(
        functools.partial(kernel, n_row, n_grp),
        out_shape=(pltpu.VMEM(block, jnp.float32), pltpu.VMEM(block, jnp.float32)),
        in_specs=[pl.BlockSpec(memory_space=pl.ANY)] * 6,
        out_specs=(pl.BlockSpec(memory_space=pltpu.VMEM), pl.BlockSpec(memory_space=pltpu.VMEM)),
        scratch_shapes=[
            pltpu.VMEM((2, *block), jnp.float32),
            pltpu.VMEM((3, total), jnp.float32),
            pltpu.VMEM((1, total), jnp.float32),
            pltpu.VMEM((2 * cols + 1, width), jnp.float32),
            pltpu.VMEM((2, 3, TILE, TILE), jnp.float32),
            pltpu.VMEM((total, 2 * width), jnp.bfloat16),
            pltpu.VMEM((total, 2 * width), jnp.bfloat16),
            pltpu.VMEM((n_row, 2 * cols + 1, width), jnp.float32),
            pltpu.VMEM((n_grp, 2 * cols, width), jnp.float32),
            pltpu.VMEM((cols, 2 * cols, width), jnp.float32),
        ],
        compiler_params=pltpu.CompilerParams(collective_id=0, has_side_effects=True),
    )(positions, detuning.reshape(1, total), populations.reshape(1, width), section.reshape(2 * cols, width), base, accum)
    return pl.pallas_call(
        store,
        out_shape=(jax.ShapeDtypeStruct(block, jnp.float32),) * 2,
        in_specs=[pl.BlockSpec(memory_space=pltpu.VMEM)] * 2,
        out_specs=(pl.BlockSpec(memory_space=pltpu.HBM),) * 2,
    )(*[pltpu.with_memory_space_constraint(r, pltpu.VMEM) for r in results])


def solution(mesh):
    return jax.shard_map(
        local,
        mesh=mesh,
        in_specs=(
            P(),
            P(),
            P("row"),
            P(None, "grp", "row"),
            P(None, "grp", "row"),
            P(None, "grp", "row"),
        ),
        out_specs=(P(None, "grp", "row"), P(None, "grp", "row")),
        check_vma=False,
    )
```

profile of v0, /device:TPU:0, one launch (start us, length us, event | category | flops | bytes accessed | tf_op | source)
XLA Modules:
  0.0 8.4 jit_solution(17641372658844660588)
XLA Ops:
  0.6 7.2 %shard_map.77 = (f32[2,16,128]{2,1,0:T(8,128)S(1)}, f32[2,16,128]{2,1,0:T(8,128)S(1)}) custom-call(f32[3,1024]{1,0:T(4,128)} %pos_in.1, f32[1,1024]{1,0:T(1,128)} %bitcast.4, f32[1,128]{1,0:T(1,128)} %bitcast.5, f32[32,128]{1,0:T(8,128)} %bitcast.3, f32[2,16,128]{2,1,0:T(8,128)} %base_in.1, f32[2,16,128]{2,1,0:T(8,128)} %accum_in.1), custom_call_target="tpu_custom_call" | custom-call | tf_op jit(solution)/shard_map/pallas_call | solution.py:503
  7.8 0.6 %shard_map.78 = (f32[2,16,128]{2,1,0:T(8,128)}, f32[2,16,128]{2,1,0:T(8,128)}) custom-call(f32[2,16,128]{2,1,0:T(8,128)S(1)} %get-tuple-element.4.next_ref, f32[2,16,128]{2,1,0:T(8,128)S(1)} %get-tuple-element.5.accum_ref), custom_call_target="tpu_custom_call" | custom-call | tf_op jit(solution)/shard_map/pallas_call | solution.py:522
where the time goes:
time: 8.58 us; the launch traced here: 8.41 us
  Pallas kernels  7.77 us (91%)
  between operations  0.63 us (7%)
    pallas_call x1, Pallas kernels, local(): pl.pallas_call(functools.partial(kernel, n_row, n_grp), out_shape=(pltpu....  7.16 us
    pallas_call x1, Pallas kernels, local(): pl.pallas_call(store, out_shape=(jax.ShapeDtypeStruct(block, jnp.float32)...  0.61 us

commit v1 on v0

--- a/solution.py
+++ b/solution.py
@@ -132,7 +132,7 @@
                 stage,
                 row_buf.at[me],
                 send_sem.at[0],
-                row_recv.at[jnp.where(me < last, 0, 1)],
+                row_recv.at[pair],
                 device_id={"row": p},
                 device_id_type=MESH,
             ).start()
@@ -201,8 +201,7 @@
 
     @pl.when((met > 0) & jnp.logical_not(ahead))
     def _():
-        with jax.named_scope("bar"):
-            pl.semaphore_wait(barrier, met)
+        pl.semaphore_wait(barrier, met)
 
     send_grp(0, jnp.where(even & jnp.logical_not(ahead), low, 0), sec_in)
 
@@ -226,8 +225,7 @@
         answer_lower(low, mine)
 
     def hear_between():
-        with jax.named_scope("wmid"):
-            pl.semaphore_wait(row_ready.at[GO], last - 2)
+        pl.semaphore_wait(row_ready.at[GO], last - 2)
 
         @pl.when(odd == 1)
         def _():
@@ -237,15 +235,13 @@
     def _():
         hear_between()
 
-    with jax.named_scope("load"):
-        pos_load.wait()
-        arrived(stage, load_sem.at[0])
+    pos_load.wait()
+    arrived(stage, load_sem.at[0])
     send_row(jnp.where(in_first, 2, 0), jnp.where(in_first, jnp.where(mine == 0, last, 2), before))
 
     @pl.when(even)
     def _():
-        with jax.named_scope("word"):
-            pl.semaphore_wait(row_ready.at[WORD], 1)
+        pl.semaphore_wait(row_ready.at[WORD], 1)
         answer_lower(low, mine)
         send_grp(low, mine, slab_part)
 
@@ -284,28 +280,27 @@
     def tile_at(j):
         return lax.rem(first + j, total)
 
-    with jax.named_scope("couple"):
-        def lower_from_odd():
-            @pl.when(jnp.logical_not(even))
-            def _():
-                send_grp(0, mine, slab_part)
-
-        def step(j, carry):
-            spread(tile_at(j + 1), lax.rem(j + 1, 2))
-            fill(tile_at(j), lax.rem(j, 2), None)
-            return carry
-
-        flat = total <= 16
-        spread(first, 0)
-        for j in range(total if flat else tiles):
-            if j == tiles + PAUSE:
-                lower_from_odd()
-            if j + 1 < total:
-                spread(tile_at(j + 1), (j + 1) % 2)
-            fill(tile_at(j), j % 2, sub_ids + j * TILE == lane_ids if j < tiles else None)
-        if not flat:
+    def lower_from_odd():
+        @pl.when(jnp.logical_not(even))
+        def _():
+            send_grp(0, mine, slab_part)
+
+    def step(j, carry):
+        spread(tile_at(j + 1), lax.rem(j + 1, 2))
+        fill(tile_at(j), lax.rem(j, 2), None)
+        return carry
+
+    flat = total <= 16
+    spread(first, 0)
+    for j in range(total if flat else tiles):
+        if j == tiles + PAUSE:
             lower_from_odd()
-            lax.fori_loop(tiles, total, step, 0)
+        if j + 1 < total:
+            spread(tile_at(j + 1), (j + 1) % 2)
+        fill(tile_at(j), j % 2, sub_ids + j * TILE == lane_ids if j < tiles else None)
+    if not flat:
+        lower_from_odd()
+        lax.fori_loop(tiles, total, step, 0)
 
     @pl.when(in_first & (mine > 0) & (last > 2))
     def _():
@@ -314,27 +309,23 @@
 
     @pl.when(between)
     def _():
-        with jax.named_scope("wgo"):
-            pl.semaphore_wait(row_ready.at[GO], 1)
+        pl.semaphore_wait(row_ready.at[GO], 1)
         send_row(2, 2 * pair)
         send_row(2 * pair + 2, last)
 
     @pl.when(mine < n_grp - 1)
     def _():
-        with jax.named_scope("ansnext"):
-            pl.semaphore_wait(grp_ready.at[NEXT], 1)
+        pl.semaphore_wait(grp_ready.at[NEXT], 1)
         send_grp(mine + 1, mine + 2, slab_part)
 
     @pl.when(jnp.logical_not(in_last))
     def _():
-        with jax.named_scope("wlate"):
-            pl.semaphore_wait(row_ready.at[LATE], 2)
+        pl.semaphore_wait(row_ready.at[LATE], 2)
         send_row(last, n_row)
 
     @pl.when(mine < n_grp - 2)
     def _():
-        with jax.named_scope("ansrest"):
-            pl.semaphore_wait(grp_ready.at[REST], n_grp - 2 - mine)
+        pl.semaphore_wait(grp_ready.at[REST], n_grp - 2 - mine)
         send_grp(mine + 2, n_grp, slab_part)
 
     det_load.wait()
@@ -370,17 +361,14 @@
     group = 2
     for lead in range(0, n_row, group):
         his, los = [], []
-        for at, count in ((0, last), (last, 2)):
-            if lead == at:
-                with jax.named_scope(f"wrow{lead}"):
-
-                    @pl.when(in_last == (at == last))
-                    def _():
-                        arrived(row_buf.at[0 : count - 1], row_recv.at[at // last])
-
-                    @pl.when(in_last != (at == last))
-                    def _():
-                        arrived(row_buf.at[0:count], row_recv.at[at // last])
+
+        @pl.when(pair == lead // group)
+        def _():
+            arrived(row_buf.at[0], row_recv.at[lead // group])
+
+        @pl.when(pair != lead // group)
+        def _():
+            arrived(row_buf.at[0:group], row_recv.at[lead // group])
 
         for p in range(lead, lead + group):
             hi, lo = left(row_buf[p])
@@ -404,15 +392,14 @@
 
     top = n_grp - 1
     if n_grp > 2:
-        with jax.named_scope("wgrp"):
-
-            @pl.when(mine < top)
-            def _():
-                arrived(grp_buf.at[0 : top - 1], grp_recv.at[0])
-
-            @pl.when(mine == top)
-            def _():
-                arrived(grp_buf.at[0:top], grp_recv.at[0])
+
+        @pl.when(mine < top)
+        def _():
+            arrived(grp_buf.at[0 : top - 1], grp_recv.at[0])
+
+        @pl.when(mine == top)
+        def _():
+            arrived(grp_buf.at[0:top], grp_recv.at[0])
 
     elif n_grp == 2:
 
@@ -433,20 +420,13 @@
         next_ref[i] = olds[0, i] + 0.5 * TIME_STEP * rate
         accum_ref[i] = olds[1, i] + TIME_STEP / 3.0 * rate
 
-    with jax.named_scope("drain"):
-        arrived(row_buf.at[0 : n_row - 1], send_sem.at[0])
-        arrived(grp_buf.at[0 : n_grp - 1], send_sem.at[1])
-
-
-def finish(n_grp, next_ref, accum_ref, grp_buf, coef, grp_recv):
-    cols, width = coef.shape[0], coef.shape[2]
-    mine, top = lax.axis_index("grp"), n_grp - 1
-
-    with jax.named_scope("wtop"):
-
-        @pl.when(mine < top)
-        def _():
-            pltpu.make_async_copy(grp_buf.at[0], grp_buf.at[0], grp_recv.at[1]).wait()
+    arrived(row_buf.at[0 : n_row - 1], send_sem.at[0])
+    arrived(grp_buf.at[0 : n_grp - 1], send_sem.at[1])
+
+
+    @pl.when(mine < top)
+    def _():
+        arrived(grp_buf.at[0], grp_recv.at[1])
 
     sums = [[jnp.zeros((cols, width), jnp.float32)] * 4 for _ in range(2)]
     for j in range(cols):
@@ -465,19 +445,15 @@
         accum_ref[i] = accum_ref[i] + TIME_STEP / 3.0 * rate
 
 
-def kernel(n_row, n_grp, pos_in, det_in, pop_in, sec_in, base_in, accum_in, next_ref, accum_ref, olds, pos_ref, det_ref, stage, wide, rhs_hi, rhs_lo, row_buf, grp_buf, coef):
-    def scope(row_recv, grp_recv, row_ready, grp_ready, load_sem, send_sem):
-        exchange(n_row=n_row, n_grp=n_grp, pos_in=pos_in, det_in=det_in, pop_in=pop_in, sec_in=sec_in, base_in=base_in, accum_in=accum_in, next_ref=next_ref, accum_ref=accum_ref, olds=olds, pos_ref=pos_ref, det_ref=det_ref, stage=stage, wide=wide, rhs_hi=rhs_hi, rhs_lo=rhs_lo, row_buf=row_buf, grp_buf=grp_buf, coef=coef, row_recv=row_recv, grp_recv=grp_recv, row_ready=row_ready, grp_ready=grp_ready, load_sem=load_sem, send_sem=send_sem)
-        finish(n_grp, next_ref, accum_ref, grp_buf, coef, grp_recv)
-
+def kernel(n_row, n_grp, *refs):
     pl.run_scoped(
-        scope,
-        row_recv=pltpu.SemaphoreType.DMA((2,)),
+        functools.partial(exchange, n_row, n_grp, *refs),
+        send_sem=pltpu.SemaphoreType.DMA((2,)),
+        row_recv=pltpu.SemaphoreType.DMA((n_row // 2,)),
         grp_recv=pltpu.SemaphoreType.DMA((2,)),
         row_ready=pltpu.SemaphoreType.REGULAR((3,)),
         grp_ready=pltpu.SemaphoreType.REGULAR((2,)),
         load_sem=pltpu.SemaphoreType.DMA((4,)),
-        send_sem=pltpu.SemaphoreType.DMA((2,)),
     )
 
 

time: 8.58 us -> 8.58 us (level)
  no operation moved by 1% of the time
where the time goes in v1:
time: 8.58 us; the launch traced here: 8.41 us
  Pallas kernels  7.77 us (91%)
  between operations  0.63 us (7%)
    pallas_call x1, Pallas kernels, local(): pl.pallas_call(functools.partial(kernel, n_row, n_grp), out_shape=(pltpu....  7.16 us
    pallas_call x1, Pallas kernels, local(): pl.pallas_call(store, out_shape=(jax.ShapeDtypeStruct(block, jnp.float32)...  0.61 us

profile of v1, /device:TPU:0, one launch (start us, length us, event | category | flops | bytes accessed | tf_op | source)
XLA Modules:
  0.0 8.4 jit_solution(7872621338139996019)
XLA Ops:
  0.6 7.2 %shard_map.77 = (f32[2,16,128]{2,1,0:T(8,128)S(1)}, f32[2,16,128]{2,1,0:T(8,128)S(1)}) custom-call(f32[3,1024]{1,0:T(4,128)} %refs_0_.1, f32[1,1024]{1,0:T(1,128)} %bitcast.4, f32[1,128]{1,0:T(1,128)} %bitcast.5, f32[32,128]{1,0:T(8,128)} %bitcast.3, f32[2,16,128]{2,1,0:T(8,128)} %refs_4_.1, f32[2,16,128]{2,1,0:T(8,128)} %refs_5_.1), custom_call_target="tpu_custom_call" | custom-call | tf_op jit(solution)/shard_map/pallas_call | solution.py:479
  7.8 0.6 %shard_map.78 = (f32[2,16,128]{2,1,0:T(8,128)}, f32[2,16,128]{2,1,0:T(8,128)}) custom-call(f32[2,16,128]{2,1,0:T(8,128)S(1)} %get-tuple-element.4.next_ref, f32[2,16,128]{2,1,0:T(8,128)S(1)} %get-tuple-element.5.accum_ref), custom_call_target="tpu_custom_call" | custom-call | tf_op jit(solution)/shard_map/pallas_call | solution.py:498

commit v2 on v1

--- a/solution.py
+++ b/solution.py
@@ -97,6 +97,23 @@
     slab = cols * n_grp
     barrier = pltpu.get_barrier_semaphore()
 
+    def grp_copy(p, source):
+        return pltpu.make_async_remote_copy(
+            source,
+            grp_buf.at[mine],
+            send_sem.at[1],
+            grp_recv.at[jnp.where(mine < n_grp - 1, 0, 1)],
+            device_id={"grp": p},
+            device_id_type=MESH,
+        )
+
+    ahead = (me == 0) & (mine > 0)
+
+    @pl.when(ahead)
+    def _():
+        pl.semaphore_wait(barrier, 1)
+        grp_copy(0, sec_in).start()
+
     last = n_row - 2
     pair = me // 2
     odd = lax.rem(me, 2)
@@ -106,7 +123,6 @@
     between = jnp.logical_not(in_first | in_last)
     even = odd == 0
     low = jnp.minimum(mine, 1)
-    ahead = in_first & even & (mine > 0)
     GO, LATE, WORD = 0, 1, 2
     NEXT, REST = 0, 1
 
@@ -142,25 +158,13 @@
 
     def send_grp(lo, hi, source):
         def body(p, carry):
-            pltpu.make_async_remote_copy(
-                source,
-                grp_buf.at[mine],
-                send_sem.at[1],
-                grp_recv.at[jnp.where(mine < n_grp - 1, 0, 1)],
-                device_id={"grp": p},
-                device_id_type=MESH,
-            ).start()
+            grp_copy(p, source).start()
             return carry
 
         lax.fori_loop(lo, hi, body, 0)
 
     def arrived(part, sem):
         pltpu.make_async_copy(part, part, sem).wait()
-
-    @pl.when(ahead)
-    def _():
-        pl.semaphore_wait(barrier, 1)
-        send_grp(0, 1, sec_in)
 
     section_loads = [
         pltpu.make_async_copy(src, dst, load_sem.at[0])

time: 8.58 us -> 8.55 us (level)
  no operation moved by 1% of the time
where the time goes in v2:
time: 8.55 us; the launch traced here: 8.39 us
  Pallas kernels  7.76 us (91%)
  between operations  0.63 us (7%)
    pallas_call x1, Pallas kernels, local(): pl.pallas_call(functools.partial(kernel, n_row, n_grp), out_shape=(pltpu....  7.15 us
    pallas_call x1, Pallas kernels, local(): pl.pallas_call(store, out_shape=(jax.ShapeDtypeStruct(block, jnp.float32)...  0.61 us

profile of v2, /device:TPU:0, one launch (start us, length us, event | category | flops | bytes accessed | tf_op | source)
XLA Modules:
  0.0 8.4 jit_solution(9250990175183181524)
XLA Ops:
  0.6 7.1 %shard_map.77 = (f32[2,16,128]{2,1,0:T(8,128)S(1)}, f32[2,16,128]{2,1,0:T(8,128)S(1)}) custom-call(f32[3,1024]{1,0:T(4,128)} %refs_0_.1, f32[1,1024]{1,0:T(1,128)} %bitcast.4, f32[1,128]{1,0:T(1,128)} %bitcast.5, f32[32,128]{1,0:T(8,128)} %bitcast.3, f32[2,16,128]{2,1,0:T(8,128)} %refs_4_.1, f32[2,16,128]{2,1,0:T(8,128)} %refs_5_.1), custom_call_target="tpu_custom_call" | custom-call | tf_op jit(solution)/shard_map/pallas_call | solution.py:483
  7.8 0.6 %shard_map.78 = (f32[2,16,128]{2,1,0:T(8,128)}, f32[2,16,128]{2,1,0:T(8,128)}) custom-call(f32[2,16,128]{2,1,0:T(8,128)S(1)} %get-tuple-element.4.next_ref, f32[2,16,128]{2,1,0:T(8,128)S(1)} %get-tuple-element.5.accum_ref), custom_call_target="tpu_custom_call" | custom-call | tf_op jit(solution)/shard_map/pallas_call | solution.py:502

commit v3 on v2

--- a/solution.py
+++ b/solution.py
@@ -13,6 +13,7 @@
 TILE = 128
 AMPLITUDE = -0.75
 PAUSE = 1
+PIECES = 4
 
 HALF_SIN = (4.442882834149929, -7.308241154546326, 3.606288958225646, -0.8457635961475002, 0.10920575363724722)
 HALF_COS = (1.4142134965650124, -6.97885098823893, 5.739461170681154, -1.8835629872981716, 0.31069819180355424)
@@ -97,22 +98,27 @@
     slab = cols * n_grp
     barrier = pltpu.get_barrier_semaphore()
 
-    def grp_copy(p, source):
-        return pltpu.make_async_remote_copy(
-            source,
-            grp_buf.at[mine],
-            send_sem.at[1],
-            grp_recv.at[jnp.where(mine < n_grp - 1, 0, 1)],
-            device_id={"grp": p},
-            device_id_type=MESH,
-        )
+    top = n_grp - 1
+    piece = 2 * cols // PIECES
+
+    def send_pieces(p, source):
+        for q in range(PIECES):
+            part = slice(q * piece, (q + 1) * piece)
+            pltpu.make_async_remote_copy(
+                source.at[part],
+                grp_buf.at[mine, part],
+                send_sem.at[1],
+                grp_recv.at[jnp.where(mine < top, 0, 1 + q)],
+                device_id={"grp": p},
+                device_id_type=MESH,
+            ).start()
 
     ahead = (me == 0) & (mine > 0)
 
     @pl.when(ahead)
     def _():
         pl.semaphore_wait(barrier, 1)
-        grp_copy(0, sec_in).start()
+        send_pieces(0, sec_in)
 
     last = n_row - 2
     pair = me // 2
@@ -158,7 +164,7 @@
 
     def send_grp(lo, hi, source):
         def body(p, carry):
-            grp_copy(p, source).start()
+            send_pieces(p, source)
             return carry
 
         lax.fori_loop(lo, hi, body, 0)
@@ -178,8 +184,14 @@
     old_loads = [
         pltpu.make_async_copy(src, olds.at[i], load_sem.at[3]) for i, src in enumerate((base_in, accum_in))
     ]
-    for load in (*section_loads, pos_load, det_load, *old_loads):
-        load.start()
+
+    def start_loads():
+        for load in (*section_loads, pos_load, det_load, *old_loads):
+            load.start()
+
+    @pl.when(jnp.logical_not(ahead))
+    def _():
+        start_loads()
 
     @pl.when(even & (mine > 0))
     def _():
@@ -199,6 +211,10 @@
 
     after = jnp.where(in_first, 2, jnp.where(in_last, n_row, last))
     to_row(barrier, after, n_row)
+
+    @pl.when(ahead)
+    def _():
+        start_loads()
 
     before = jnp.where(in_first, 0, jnp.where(in_last, last, 2))
     met = before + jnp.where(even, low, 1 + mine + mine - low)
@@ -394,7 +410,6 @@
     z_real = z_real + total_shift * y_real + 0.5 * y_imag
     z_imag = z_imag + total_shift * y_imag - 0.5 * y_real
 
-    top = n_grp - 1
     if n_grp > 2:
 
         @pl.when(mine < top)
@@ -427,23 +442,23 @@
     arrived(row_buf.at[0 : n_row - 1], send_sem.at[0])
     arrived(grp_buf.at[0 : n_grp - 1], send_sem.at[1])
 
-
-    @pl.when(mine < top)
-    def _():
-        arrived(grp_buf.at[0], grp_recv.at[1])
-
-    sums = [[jnp.zeros((cols, width), jnp.float32)] * 4 for _ in range(2)]
-    for j in range(cols):
-        fr = grp_buf[top, j : j + 1]
-        fi = grp_buf[top, cols + j : cols + j + 1]
-        wr, wi = coef[j, :cols], coef[j, cols:]
-        k = 2 * (j % 2)
-        sums[0][k] = sums[0][k] + wr * fr
-        sums[0][k + 1] = sums[0][k + 1] + wi * fi
-        sums[1][k] = sums[1][k] + wr * fi
-        sums[1][k + 1] = sums[1][k + 1] + wi * fr
-    v_real = (sums[0][0] + sums[0][1]) + (sums[0][2] + sums[0][3])
-    v_imag = (sums[1][0] + sums[1][2]) - (sums[1][1] + sums[1][3])
+    v_real = v_imag = jnp.zeros((cols, width), jnp.float32)
+    for q in range(PIECES):
+
+        @pl.when(mine < top)
+        def _():
+            arrived(grp_buf.at[0, 0:piece], grp_recv.at[1 + q])
+
+        for row in range(q * piece, (q + 1) * piece):
+            j = row % cols
+            f = grp_buf[top, row : row + 1]
+            wr, wi = coef[j, :cols], coef[j, cols:]
+            if row < cols:
+                v_real = v_real + wr * f
+                v_imag = v_imag - wi * f
+            else:
+                v_real = v_real + wi * f
+                v_imag = v_imag + wr * f
     for i, rate in enumerate((-v_imag, v_real)):
         next_ref[i] = next_ref[i] + 0.5 * TIME_STEP * rate
         accum_ref[i] = accum_ref[i] + TIME_STEP / 3.0 * rate
@@ -454,7 +469,7 @@
         functools.partial(exchange, n_row, n_grp, *refs),
         send_sem=pltpu.SemaphoreType.DMA((2,)),
         row_recv=pltpu.SemaphoreType.DMA((n_row // 2,)),
-        grp_recv=pltpu.SemaphoreType.DMA((2,)),
+        grp_recv=pltpu.SemaphoreType.DMA((1 + PIECES,)),
         row_ready=pltpu.SemaphoreType.REGULAR((3,)),
         grp_ready=pltpu.SemaphoreType.REGULAR((2,)),
         load_sem=pltpu.SemaphoreType.DMA((4,)),

time: 8.55 us -> 8.49 us (level)
  no operation moved by 1% of the time
where the time goes in v3:
time: 8.49 us; the launch traced here: 8.34 us
  Pallas kernels  7.71 us (91%)
  between operations  0.63 us (7%)
    pallas_call x1, Pallas kernels, local(): pl.pallas_call(functools.partial(kernel, n_row, n_grp), out_shape=(pltpu....  7.1 us
    pallas_call x1, Pallas kernels, local(): pl.pallas_call(store, out_shape=(jax.ShapeDtypeStruct(block, jnp.float32)...  0.61 us

profile of v3, /device:TPU:0, one launch (start us, length us, event | category | flops | bytes accessed | tf_op | source)
XLA Modules:
  0.0 8.3 jit_solution(3232108209549052179)
XLA Ops:
  0.6 7.1 %shard_map.77 = (f32[2,16,128]{2,1,0:T(8,128)S(1)}, f32[2,16,128]{2,1,0:T(8,128)S(1)}) custom-call(f32[3,1024]{1,0:T(4,128)} %refs_0_.1, f32[1,1024]{1,0:T(1,128)} %bitcast.4, f32[1,128]{1,0:T(1,128)} %bitcast.5, f32[32,128]{1,0:T(8,128)} %bitcast.3, f32[2,16,128]{2,1,0:T(8,128)} %refs_4_.1, f32[2,16,128]{2,1,0:T(8,128)} %refs_5_.1), custom_call_target="tpu_custom_call" | custom-call | tf_op jit(solution)/shard_map/pallas_call | solution.py:498
  7.7 0.6 %shard_map.78 = (f32[2,16,128]{2,1,0:T(8,128)}, f32[2,16,128]{2,1,0:T(8,128)}) custom-call(f32[2,16,128]{2,1,0:T(8,128)S(1)} %get-tuple-element.4.next_ref, f32[2,16,128]{2,1,0:T(8,128)S(1)} %get-tuple-element.5.accum_ref), custom_call_target="tpu_custom_call" | custom-call | tf_op jit(solution)/shard_map/pallas_call | solution.py:517

commit v4 on v3

--- a/solution.py
+++ b/solution.py
@@ -12,7 +12,7 @@
 PAD = 16
 TILE = 128
 AMPLITUDE = -0.75
-PAUSE = 1
+PAUSE = 3
 PIECES = 4
 
 HALF_SIN = (4.442882834149929, -7.308241154546326, 3.606288958225646, -0.8457635961475002, 0.10920575363724722)
@@ -263,7 +263,7 @@
     def _():
         pl.semaphore_wait(row_ready.at[WORD], 1)
         answer_lower(low, mine)
-        send_grp(low, mine, slab_part)
+        send_grp(low, jnp.where(ahead, low, mine), slab_part)
 
     send_row(partner, partner + 1)
 
@@ -321,6 +321,10 @@
     if not flat:
         lower_from_odd()
         lax.fori_loop(tiles, total, step, 0)
+
+    @pl.when(ahead)
+    def _():
+        send_grp(1, mine, slab_part)
 
     @pl.when(in_first & (mine > 0) & (last > 2))
     def _():
@@ -376,10 +380,39 @@
         signed = jnp.broadcast_to(2.0 * slab_and_pop[2 * cols :] - 1.0, (PAD, width))
         return split(jnp.concatenate([slab_and_pop[: 2 * cols], signed], axis=0))
 
+    def lower_planes():
+        if n_grp > 2:
+
+            @pl.when(mine < top)
+            def _():
+                arrived(grp_buf.at[0 : top - 1], grp_recv.at[0])
+
+            @pl.when(mine == top)
+            def _():
+                arrived(grp_buf.at[0:top], grp_recv.at[0])
+
+        elif n_grp == 2:
+
+            @pl.when(mine == top)
+            def _():
+                arrived(grp_buf.at[0:top], grp_recv.at[0])
+
+        blocks = [grp_buf[g] for g in range(top)]
+        full = jnp.concatenate(
+            [jnp.concatenate([block[:cols], block[cols:]], axis=1) for block in blocks], axis=0
+        )
+        f_hi, f_lo = split(full)
+        v = bdot(l_hi, f_hi) + bdot(l_lo, f_hi) + bdot(l_hi, f_lo)
+        v_imag = v[:cols, width:] - v[cols:, :width]
+        v_real = v[:cols, :width] + v[cols:, width:]
+        return v_real, v_imag
+
     main = jnp.zeros((4 * cols + 2 * PAD, 2 * width), jnp.float32)
     rest = jnp.zeros((2 * cols + PAD, 2 * width), jnp.float32)
     group = 2
     for lead in range(0, n_row, group):
+        if lead == last:
+            v_real, v_imag = lower_planes()
         his, los = [], []
 
         @pl.when(pair == lead // group)
@@ -410,30 +443,8 @@
     z_real = z_real + total_shift * y_real + 0.5 * y_imag
     z_imag = z_imag + total_shift * y_imag - 0.5 * y_real
 
-    if n_grp > 2:
-
-        @pl.when(mine < top)
-        def _():
-            arrived(grp_buf.at[0 : top - 1], grp_recv.at[0])
-
-        @pl.when(mine == top)
-        def _():
-            arrived(grp_buf.at[0:top], grp_recv.at[0])
-
-    elif n_grp == 2:
-
-        @pl.when(mine == top)
-        def _():
-            arrived(grp_buf.at[0:top], grp_recv.at[0])
-
-    blocks = [grp_buf[g] for g in range(top)]
-    full = jnp.concatenate(
-        [jnp.concatenate([block[:cols], block[cols:]], axis=1) for block in blocks], axis=0
-    )
-    f_hi, f_lo = split(full)
-    v = bdot(l_hi, f_hi) + bdot(l_lo, f_hi) + bdot(l_hi, f_lo)
-    z_imag = z_imag - (v[:cols, width:] - v[cols:, :width])
-    z_real = z_real - (v[:cols, :width] + v[cols:, width:])
+    z_imag = z_imag - v_imag
+    z_real = z_real - v_real
 
     for i, rate in enumerate((z_imag, -z_real)):
         next_ref[i] = olds[0, i] + 0.5 * TIME_STEP * rate

time: 8.49 us -> 8.45 us (level)
  no operation moved by 1% of the time
where the time goes in v4:
time: 8.45 us; the launch traced here: 8.3 us
  Pallas kernels  7.67 us (91%)
  between operations  0.63 us (7%)
    pallas_call x1, Pallas kernels, local(): pl.pallas_call(functools.partial(kernel, n_row, n_grp), out_shape=(pltpu....  7.06 us
    pallas_call x1, Pallas kernels, local(): pl.pallas_call(store, out_shape=(jax.ShapeDtypeStruct(block, jnp.float32)...  0.61 us

profile of v4, /device:TPU:0, one launch (start us, length us, event | category | flops | bytes accessed | tf_op | source)
XLA Modules:
  0.0 8.3 jit_solution(8073763571803282134)
XLA Ops:
  0.6 7.1 %shard_map.77 = (f32[2,16,128]{2,1,0:T(8,128)S(1)}, f32[2,16,128]{2,1,0:T(8,128)S(1)}) custom-call(f32[3,1024]{1,0:T(4,128)} %refs_0_.1, f32[1,1024]{1,0:T(1,128)} %bitcast.4, f32[1,128]{1,0:T(1,128)} %bitcast.5, f32[32,128]{1,0:T(8,128)} %bitcast.3, f32[2,16,128]{2,1,0:T(8,128)} %refs_4_.1, f32[2,16,128]{2,1,0:T(8,128)} %refs_5_.1), custom_call_target="tpu_custom_call" | custom-call | tf_op jit(solution)/shard_map/pallas_call | solution.py:509
  7.7 0.6 %shard_map.78 = (f32[2,16,128]{2,1,0:T(8,128)}, f32[2,16,128]{2,1,0:T(8,128)}) custom-call(f32[2,16,128]{2,1,0:T(8,128)S(1)} %get-tuple-element.4.next_ref, f32[2,16,128]{2,1,0:T(8,128)S(1)} %get-tuple-element.5.accum_ref), custom_call_target="tpu_custom_call" | custom-call | tf_op jit(solution)/shard_map/pallas_call | solution.py:528

commit v5 on v4

--- a/solution.py
+++ b/solution.py
@@ -267,6 +267,10 @@
 
     send_row(partner, partner + 1)
 
+    @pl.when(jnp.logical_not(even) & (mine < top))
+    def _():
+        send_grp(0, mine, slab_part)
+
     my_start = pl.multiple_of(me * width, width)
     rows = [pos_ref[d : d + 1, pl.ds(my_start, width)] for d in range(3)]
     tiles = width // TILE
@@ -301,7 +305,7 @@
         return lax.rem(first + j, total)
 
     def lower_from_odd():
-        @pl.when(jnp.logical_not(even))
+        @pl.when(jnp.logical_not(even) & (mine == top))
         def _():
             send_grp(0, mine, slab_part)
 

time: 8.45 us -> 8.45 us (level)
  no operation moved by 1% of the time
where the time goes in v5:
time: 8.45 us; the launch traced here: 8.3 us
  Pallas kernels  7.67 us (91%)
  between operations  0.63 us (7%)
    pallas_call x1, Pallas kernels, local(): pl.pallas_call(functools.partial(kernel, n_row, n_grp), out_shape=(pltpu....  7.06 us
    pallas_call x1, Pallas kernels, local(): pl.pallas_call(store, out_shape=(jax.ShapeDtypeStruct(block, jnp.float32)...  0.61 us

profile of v5, /device:TPU:0, one launch (start us, length us, event | category | flops | bytes accessed | tf_op | source)
XLA Modules:
  0.0 8.3 jit_solution(10226006405646223038)
XLA Ops:
  0.6 7.1 %shard_map.77 = (f32[2,16,128]{2,1,0:T(8,128)S(1)}, f32[2,16,128]{2,1,0:T(8,128)S(1)}) custom-call(f32[3,1024]{1,0:T(4,128)} %refs_0_.1, f32[1,1024]{1,0:T(1,128)} %bitcast.4, f32[1,128]{1,0:T(1,128)} %bitcast.5, f32[32,128]{1,0:T(8,128)} %bitcast.3, f32[2,16,128]{2,1,0:T(8,128)} %refs_4_.1, f32[2,16,128]{2,1,0:T(8,128)} %refs_5_.1), custom_call_target="tpu_custom_call" | custom-call | tf_op jit(solution)/shard_map/pallas_call | solution.py:513
  7.7 0.6 %shard_map.78 = (f32[2,16,128]{2,1,0:T(8,128)}, f32[2,16,128]{2,1,0:T(8,128)}) custom-call(f32[2,16,128]{2,1,0:T(8,128)S(1)} %get-tuple-element.4.next_ref, f32[2,16,128]{2,1,0:T(8,128)S(1)} %get-tuple-element.5.accum_ref), custom_call_target="tpu_custom_call" | custom-call | tf_op jit(solution)/shard_map/pallas_call | solution.py:532

commit v6 on v5

--- a/solution.py
+++ b/solution.py
@@ -454,11 +454,12 @@
         next_ref[i] = olds[0, i] + 0.5 * TIME_STEP * rate
         accum_ref[i] = olds[1, i] + TIME_STEP / 3.0 * rate
 
-    arrived(row_buf.at[0 : n_row - 1], send_sem.at[0])
-    arrived(grp_buf.at[0 : n_grp - 1], send_sem.at[1])
 
     v_real = v_imag = jnp.zeros((cols, width), jnp.float32)
     for q in range(PIECES):
+        if q == PIECES - 1:
+            arrived(row_buf.at[0 : n_row - 1], send_sem.at[0])
+            arrived(grp_buf.at[0 : n_grp - 1], send_sem.at[1])
 
         @pl.when(mine < top)
         def _():

time: 8.45 us -> 8.45 us (level)
  no operation moved by 1% of the time
where the time goes in v6:
time: 8.45 us; the launch traced here: 8.3 us
  Pallas kernels  7.67 us (91%)
  between operations  0.63 us (7%)
    pallas_call x1, Pallas kernels, local(): pl.pallas_call(functools.partial(kernel, n_row, n_grp), out_shape=(pltpu....  7.06 us
    pallas_call x1, Pallas kernels, local(): pl.pallas_call(store, out_shape=(jax.ShapeDtypeStruct(block, jnp.float32)...  0.61 us

profile of v6, /device:TPU:0, one launch (start us, length us, event | category | flops | bytes accessed | tf_op | source)
XLA Modules:
  0.0 8.3 jit_solution(5573094365518897338)
XLA Ops:
  0.6 7.1 %shard_map.77 = (f32[2,16,128]{2,1,0:T(8,128)S(1)}, f32[2,16,128]{2,1,0:T(8,128)S(1)}) custom-call(f32[3,1024]{1,0:T(4,128)} %refs_0_.1, f32[1,1024]{1,0:T(1,128)} %bitcast.4, f32[1,128]{1,0:T(1,128)} %bitcast.5, f32[32,128]{1,0:T(8,128)} %bitcast.3, f32[2,16,128]{2,1,0:T(8,128)} %refs_4_.1, f32[2,16,128]{2,1,0:T(8,128)} %refs_5_.1), custom_call_target="tpu_custom_call" | custom-call | tf_op jit(solution)/shard_map/pallas_call | solution.py:514
  7.7 0.6 %shard_map.78 = (f32[2,16,128]{2,1,0:T(8,128)}, f32[2,16,128]{2,1,0:T(8,128)}) custom-call(f32[2,16,128]{2,1,0:T(8,128)S(1)} %get-tuple-element.4.next_ref, f32[2,16,128]{2,1,0:T(8,128)S(1)} %get-tuple-element.5.accum_ref), custom_call_target="tpu_custom_call" | custom-call | tf_op jit(solution)/shard_map/pallas_call | solution.py:533
